TPU v7x, 32 devices: a whole 2x2x4 slice. The times are simulated.
32 devices in a mesh: part: 2 (over x), data: 4 (over z), stage: 4 (over y, core).
Axes of the slice: x: 2, y: 2, z: 4, core: 2. Of those that a mesh axis runs over, the one named last changes fastest.
Arguments:
- x: bfloat16 [32, 64, 1024], P(('part', 'data')), parts along dimension 0
- g: bfloat16 [32, 64, 1024], P(('part', 'data')), parts along dimension 0
- w_in: bfloat16 [2, 4, 1024, 4096], P(None, 'stage')
- w_out: bfloat16 [2, 4, 4096, 1024], P(None, 'stage')
Outputs:
- output 1: bfloat16 [32, 64, 1024], P(('part', 'data')), parts along dimension 0
- output 2: bfloat16 [32, 64, 1024], P(('part', 'data')), parts along dimension 0
- output 3: float32 [4, 4, 1024, 4096], P('part', 'stage'), parts along dimension 0
- output 4: float32 [4, 4, 4096, 1024], P('part', 'stage'), parts along dimension 0
There are 2 independent parts. A program takes and returns all parts, laid end to end along the dimension named above; an argument that names none is the same for every part.
All inputs are finite; a program needn't handle non-finite values.
Results may differ from a plain program's by a relative error of at most 0.0176001.
Values are sent between devices in bfloat16 or wider.
A program may use at most 1 GiB of HBM per device.

v0:
```python
import functools
import jax
import jax.numpy as jnp
from jax import lax
from jax.sharding import PartitionSpec as P


def layer_forward(h_in, w_first, w_second):
    pre_act = jnp.dot(h_in, w_first, preferred_element_type=jnp.float32)
    hidden = jax.nn.gelu(pre_act, approximate=True).astype(jnp.bfloat16)
    delta_out = jnp.dot(hidden, w_second, preferred_element_type=jnp.float32)
    return (h_in.astype(jnp.float32) + delta_out).astype(jnp.bfloat16), pre_act


def layer_backward(h_in, pre_act, g_next, w_first, w_second):
    gelu_val, gelu_pull = jax.vjp(functools.partial(jax.nn.gelu, approximate=True), pre_act)
    hidden = gelu_val.astype(jnp.bfloat16)
    grad_second = jnp.einsum('tf,td->fd', hidden, g_next, preferred_element_type=jnp.float32)
    grad_hidden = jnp.einsum('td,fd->tf', g_next, w_second, preferred_element_type=jnp.float32)
    grad_pre = gelu_pull(grad_hidden)[0].astype(jnp.bfloat16)
    grad_first = jnp.einsum('td,tf->df', h_in, grad_pre, preferred_element_type=jnp.float32)
    grad_prev = jnp.einsum('tf,df->td', grad_pre, w_first, preferred_element_type=jnp.float32)
    g_prev = (g_next.astype(jnp.float32) + grad_prev).astype(jnp.bfloat16)
    return g_prev, grad_first, grad_second


def pick_row(stacked, row_idx):
    return lax.dynamic_index_in_dim(stacked, row_idx, 0, keepdims=False)


def put_row(stacked, row_val, row_idx):
    return lax.dynamic_update_index_in_dim(stacked, row_val, row_idx, 0)


def solution(mesh):
    stages = mesh.shape['stage']
    to_next = [(source_idx, (source_idx + 1) % stages) for source_idx in range(stages)]
    to_prev = [(source_idx, (source_idx - 1) % stages) for source_idx in range(stages)]

    def local_fn(x, g, w_in, w_out):
        first_loc = w_in[:, 0]
        second_loc = w_out[:, 0]
        dev_layers, model_dim, hidden_dim = first_loc.shape
        micro_count, tokens = x.shape[0], x.shape[1]
        unit_count = dev_layers * micro_count
        span_size = dev_layers * stages
        tick_count = unit_count + stages - 1
        stage_idx = lax.axis_index('stage')
        is_first = stage_idx == 0
        is_last = stage_idx == stages - 1

        def fwd_tick(tick_idx, loop_state):
            incoming, h_saved, pre_saved, y_buf = loop_state
            unit_raw = tick_idx - stage_idx
            active = (unit_raw >= 0) & (unit_raw < unit_count)
            unit_idx = jnp.clip(unit_raw, 0, unit_count - 1)
            group_idx = unit_idx // span_size
            within = unit_idx % span_size
            layer_idx = within // stages
            micro_idx = group_idx * stages + within % stages

            def run_unit(buffers):
                h_saved, pre_saved, y_buf = buffers
                h_in = jnp.where(is_first & (layer_idx == 0), pick_row(x, micro_idx), incoming)
                h_out, pre_act = layer_forward(h_in, pick_row(first_loc, layer_idx), pick_row(second_loc, layer_idx))
                h_saved = put_row(h_saved, h_in, unit_idx)
                pre_saved = put_row(pre_saved, pre_act, unit_idx)
                y_new = jnp.where(is_last & (layer_idx == dev_layers - 1), h_out, pick_row(y_buf, micro_idx))
                y_buf = put_row(y_buf, y_new, micro_idx)
                return h_out, h_saved, pre_saved, y_buf

            def skip_unit(buffers):
                return (jnp.zeros((tokens, model_dim), jnp.bfloat16),) + buffers

            h_out, h_saved, pre_saved, y_buf = lax.cond(active, run_unit, skip_unit, (h_saved, pre_saved, y_buf))
            return lax.ppermute(h_out, 'stage', to_next), h_saved, pre_saved, y_buf

        fwd_init = (jnp.zeros((tokens, model_dim), jnp.bfloat16), jnp.zeros((unit_count, tokens, model_dim), jnp.bfloat16), jnp.zeros((unit_count, tokens, hidden_dim), jnp.float32), jnp.zeros_like(x))
        last_sent, h_saved, pre_saved, y_buf = lax.fori_loop(0, tick_count, fwd_tick, fwd_init)

        def bwd_tick(tick_idx, loop_state):
            incoming, acc_first, acc_second, dx_buf = loop_state
            unit_raw = tick_idx - (stages - 1 - stage_idx)
            active = (unit_raw >= 0) & (unit_raw < unit_count)
            unit_idx = jnp.clip(unit_raw, 0, unit_count - 1)
            group_idx = unit_idx // span_size
            within = unit_idx % span_size
            layer_idx = dev_layers - 1 - within // stages
            lane_idx = within % stages
            micro_idx = group_idx * stages + lane_idx
            saved_idx = group_idx * span_size + layer_idx * stages + lane_idx

            def run_unit(buffers):
                acc_first, acc_second, dx_buf = buffers
                g_next = jnp.where(is_last & (layer_idx == dev_layers - 1), pick_row(g, micro_idx), incoming)
                g_prev, grad_first, grad_second = layer_backward(pick_row(h_saved, saved_idx), pick_row(pre_saved, saved_idx), g_next, pick_row(first_loc, layer_idx), pick_row(second_loc, layer_idx))
                acc_first = put_row(acc_first, pick_row(acc_first, layer_idx) + grad_first, layer_idx)
                acc_second = put_row(acc_second, pick_row(acc_second, layer_idx) + grad_second, layer_idx)
                dx_new = jnp.where(is_first & (layer_idx == 0), g_prev, pick_row(dx_buf, micro_idx))
                dx_buf = put_row(dx_buf, dx_new, micro_idx)
                return g_prev, acc_first, acc_second, dx_buf

            def skip_unit(buffers):
                return (jnp.zeros((tokens, model_dim), jnp.bfloat16),) + buffers

            g_prev, acc_first, acc_second, dx_buf = lax.cond(active, run_unit, skip_unit, (acc_first, acc_second, dx_buf))
            return lax.ppermute(g_prev, 'stage', to_prev), acc_first, acc_second, dx_buf

        bwd_init = (jnp.zeros((tokens, model_dim), jnp.bfloat16), jnp.zeros((dev_layers, model_dim, hidden_dim), jnp.float32), jnp.zeros((dev_layers, hidden_dim, model_dim), jnp.float32), jnp.zeros_like(x))
        last_grad, acc_first, acc_second, dx_buf = lax.fori_loop(0, tick_count, bwd_tick, bwd_init)
        y_full = lax.psum(jnp.where(is_last, y_buf, jnp.zeros_like(y_buf)), 'stage')
        dx_full = lax.psum(jnp.where(is_first, dx_buf, jnp.zeros_like(dx_buf)), 'stage')
        grad_first = lax.psum(acc_first, 'data')
        grad_second = lax.psum(acc_second, 'data')
        return y_full, dx_full, grad_first[:, None], grad_second[:, None]

    spec_rows = P(('part', 'data'))
    spec_weights = P(None, 'stage')
    spec_grads = P('part', 'stage')
    return jax.shard_map(local_fn, mesh=mesh, in_specs=(spec_rows, spec_rows, spec_weights, spec_weights), out_specs=(spec_rows, spec_rows, spec_grads, spec_grads), check_vma=False)
```

profile of v0, /device:TPU:0, one launch (start us, length us, event | category | flops | bytes accessed | tf_op | source)
XLA Modules:
  0.0 3021.8 jit_solution(16545304461490899584)
XLA Ops:
  11.7 172.8 %while.44 = (s32[]{:T(128)}, bf16[64,1024]{1,0:T(8,128)(2,1)S(1)}, bf16[8,64,1024]{2,1,0:T(8,128)(2,1)S(1)}, f32[8,64,4096]{2,1,0:T(8,128)}, bf16[4,64,1024]{2,1...) while((s32[]{:T(128)}, bf16[64,1024]{1,0:T(8,128)(2,1)S(1)}, ...), condition=%wide.region_3.4_spmd, body=%wide.region_0.3_spmd.sunk | while | flops 1076428800 | bytes 21890016 | solution.py:79
  11.7 11.9 conditional.4
  28.1 11.9 conditional.4
  44.4 11.9 conditional.4
  60.8 11.9 conditional.4
  77.2 12.0 conditional.4
  93.6 11.9 conditional.4
  110.0 11.9 conditional.4
  126.3 12.0 conditional.4
  142.8 9.0 collective-permute-start
  156.8 13.8 collective-permute-done
  170.7 13.9 collective-permute-done
  185.5 11.5 broadcast_in_dim.68
  197.0 11.4 broadcast_in_dim.67
  208.4 534.7 %while.45 = (s32[]{:T(128)}, bf16[64,1024]{1,0:T(8,128)(2,1)S(1)}, f32[2,1024,4096]{2,1,0:T(8,128)}, f32[2,4096,1024]{2,1,0:T(8,128)}, bf16[4,64,1024]{2,1,0:T(8...) while((s32[]{:T(128)}, bf16[64,1024]{1,0:T(8,128)(2,1)S(1)}, ...), condition=%wide.region_8.9_spmd, body=%wide.region_5.8_spmd.sunk | while | flops 2163802112 | bytes 156763120 | solution.py:110
  208.4 44.2 %collective-permute-start.1 = (bf16[64,1024]{1,0:T(8,128)(2,1)S(1)}, bf16[64,1024]{1,0:T(8,128)(2,1)S(1)}, u32[]{:S(2)}, u32[]{:S(2)}) collective-permute-start(bf16[64,1024]{1,0:T(8,128)(2,1)S(1)} %get-tuple-element.1699), channel_id=1, source_target_pairs={{0,3},{1,0},{2,1},{3,2},{4,7},{5,4},{6,5},{7,6},{8,11},{9,8},{10,9... | collective-permute-start | bytes 393224 | tf_op jit(solution)/shard_map/while/body/eval_jaxpr/ppermute | solution.py:107
  255.2 46.8 %collective-permute-start.1 = (bf16[64,1024]{1,0:T(8,128)(2,1)S(1)}, bf16[64,1024]{1,0:T(8,128)(2,1)S(1)}, u32[]{:S(2)}, u32[]{:S(2)}) collective-permute-start(bf16[64,1024]{1,0:T(8,128)(2,1)S(1)} %get-tuple-element.1699), channel_id=1, source_target_pairs={{0,3},{1,0},{2,1},{3,2},{4,7},{5,4},{6,5},{7,6},{8,11},{9,8},{10,9... | collective-permute-start | bytes 393224 | tf_op jit(solution)/shard_map/while/body/eval_jaxpr/ppermute | solution.py:107
  304.6 46.8 %collective-permute-start.1 = (bf16[64,1024]{1,0:T(8,128)(2,1)S(1)}, bf16[64,1024]{1,0:T(8,128)(2,1)S(1)}, u32[]{:S(2)}, u32[]{:S(2)}) collective-permute-start(bf16[64,1024]{1,0:T(8,128)(2,1)S(1)} %get-tuple-element.1699), channel_id=1, source_target_pairs={{0,3},{1,0},{2,1},{3,2},{4,7},{5,4},{6,5},{7,6},{8,11},{9,8},{10,9... | collective-permute-start | bytes 393224 | tf_op jit(solution)/shard_map/while/body/eval_jaxpr/ppermute | solution.py:107
  353.9 45.0 %conditional.5 = (bf16[64,1024]{1,0:T(8,128)(2,1)S(1)}, f32[2,1024,4096]{2,1,0:T(8,128)}, f32[2,4096,1024]{2,1,0:T(8,128)}, bf16[4,64,1024]{2,1,0:T(8,128)(2,1)S(1)}) conditional(s32[]{:T(128)} %convert_element_type.92, (f32[2,1024,4096]{2,1,0:T(8,128)}, f32[2,4096,1024]{2,1,0:T(8,128)}, bf16[4,64,1024]{2,1,0:T(8,128)(2,1)S(1)}) %tuple.177, ...), branch_computations={%region_6.6_spmd, %region_7.7_spmd.clone} | conditional | flops 2163802112 | bytes 156238368 | solution.py:106
  367.4 6.6 constant_dynamic-slice_fusion.1
  374.0 8.5 bitcast_dynamic-update-slice_fusion.1
  382.5 6.6 constant_dynamic-slice_fusion
  389.1 9.8 bitcast_dynamic-update-slice_fusion
  403.3 45.0 %conditional.5 = (bf16[64,1024]{1,0:T(8,128)(2,1)S(1)}, f32[2,1024,4096]{2,1,0:T(8,128)}, f32[2,4096,1024]{2,1,0:T(8,128)}, bf16[4,64,1024]{2,1,0:T(8,128)(2,1)S(1)}) conditional(s32[]{:T(128)} %convert_element_type.92, (f32[2,1024,4096]{2,1,0:T(8,128)}, f32[2,4096,1024]{2,1,0:T(8,128)}, bf16[4,64,1024]{2,1,0:T(8,128)(2,1)S(1)}) %tuple.177, ...), branch_computations={%region_6.6_spmd, %region_7.7_spmd.clone} | conditional | flops 2163802112 | bytes 156238368 | solution.py:106
  416.7 6.6 constant_dynamic-slice_fusion.1
  423.3 8.5 bitcast_dynamic-update-slice_fusion.1
  431.9 6.6 constant_dynamic-slice_fusion
  438.4 9.8 bitcast_dynamic-update-slice_fusion
  452.6 45.0 %conditional.5 = (bf16[64,1024]{1,0:T(8,128)(2,1)S(1)}, f32[2,1024,4096]{2,1,0:T(8,128)}, f32[2,4096,1024]{2,1,0:T(8,128)}, bf16[4,64,1024]{2,1,0:T(8,128)(2,1)S(1)}) conditional(s32[]{:T(128)} %convert_element_type.92, (f32[2,1024,4096]{2,1,0:T(8,128)}, f32[2,4096,1024]{2,1,0:T(8,128)}, bf16[4,64,1024]{2,1,0:T(8,128)(2,1)S(1)}) %tuple.177, ...), branch_computations={%region_6.6_spmd, %region_7.7_spmd.clone} | conditional | flops 2163802112 | bytes 156238368 | solution.py:106
  466.1 6.6 constant_dynamic-slice_fusion.1
  472.7 8.5 bitcast_dynamic-update-slice_fusion.1
  481.2 6.6 constant_dynamic-slice_fusion
  487.8 9.8 bitcast_dynamic-update-slice_fusion
  502.0 45.0 %conditional.5 = (bf16[64,1024]{1,0:T(8,128)(2,1)S(1)}, f32[2,1024,4096]{2,1,0:T(8,128)}, f32[2,4096,1024]{2,1,0:T(8,128)}, bf16[4,64,1024]{2,1,0:T(8,128)(2,1)S(1)}) conditional(s32[]{:T(128)} %convert_element_type.92, (f32[2,1024,4096]{2,1,0:T(8,128)}, f32[2,4096,1024]{2,1,0:T(8,128)}, bf16[4,64,1024]{2,1,0:T(8,128)(2,1)S(1)}) %tuple.177, ...), branch_computations={%region_6.6_spmd, %region_7.7_spmd.clone} | conditional | flops 2163802112 | bytes 156238368 | solution.py:106
  515.4 6.6 constant_dynamic-slice_fusion.1
  522.0 8.5 bitcast_dynamic-update-slice_fusion.1
  530.6 6.6 constant_dynamic-slice_fusion
  537.1 9.8 bitcast_dynamic-update-slice_fusion
  551.3 45.0 %conditional.5 = (bf16[64,1024]{1,0:T(8,128)(2,1)S(1)}, f32[2,1024,4096]{2,1,0:T(8,128)}, f32[2,4096,1024]{2,1,0:T(8,128)}, bf16[4,64,1024]{2,1,0:T(8,128)(2,1)S(1)}) conditional(s32[]{:T(128)} %convert_element_type.92, (f32[2,1024,4096]{2,1,0:T(8,128)}, f32[2,4096,1024]{2,1,0:T(8,128)}, bf16[4,64,1024]{2,1,0:T(8,128)(2,1)S(1)}) %tuple.177, ...), branch_computations={%region_6.6_spmd, %region_7.7_spmd.clone} | conditional | flops 2163802112 | bytes 156238368 | solution.py:106
  564.8 6.6 constant_dynamic-slice_fusion.1
  571.4 8.5 bitcast_dynamic-update-slice_fusion.1
  579.9 6.6 constant_dynamic-slice_fusion
  586.5 9.8 bitcast_dynamic-update-slice_fusion
  600.7 45.0 %conditional.5 = (bf16[64,1024]{1,0:T(8,128)(2,1)S(1)}, f32[2,1024,4096]{2,1,0:T(8,128)}, f32[2,4096,1024]{2,1,0:T(8,128)}, bf16[4,64,1024]{2,1,0:T(8,128)(2,1)S(1)}) conditional(s32[]{:T(128)} %convert_element_type.92, (f32[2,1024,4096]{2,1,0:T(8,128)}, f32[2,4096,1024]{2,1,0:T(8,128)}, bf16[4,64,1024]{2,1,0:T(8,128)(2,1)S(1)}) %tuple.177, ...), branch_computations={%region_6.6_spmd, %region_7.7_spmd.clone} | conditional | flops 2163802112 | bytes 156238368 | solution.py:106
  614.1 6.6 constant_dynamic-slice_fusion.1
  620.7 8.5 bitcast_dynamic-update-slice_fusion.1
  629.3 6.6 constant_dynamic-slice_fusion
  635.9 9.8 bitcast_dynamic-update-slice_fusion
  648.2 45.0 %conditional.5 = (bf16[64,1024]{1,0:T(8,128)(2,1)S(1)}, f32[2,1024,4096]{2,1,0:T(8,128)}, f32[2,4096,1024]{2,1,0:T(8,128)}, bf16[4,64,1024]{2,1,0:T(8,128)(2,1)S(1)}) conditional(s32[]{:T(128)} %convert_element_type.92, (f32[2,1024,4096]{2,1,0:T(8,128)}, f32[2,4096,1024]{2,1,0:T(8,128)}, bf16[4,64,1024]{2,1,0:T(8,128)(2,1)S(1)}) %tuple.177, ...), branch_computations={%region_6.6_spmd, %region_7.7_spmd.clone} | conditional | flops 2163802112 | bytes 156238368 | solution.py:106
  649.1 6.4 fusion.18
  661.6 6.6 constant_dynamic-slice_fusion.1
  668.2 8.5 bitcast_dynamic-update-slice_fusion.1
  676.8 6.6 constant_dynamic-slice_fusion
  683.3 9.8 bitcast_dynamic-update-slice_fusion
  695.7 45.0 %conditional.5 = (bf16[64,1024]{1,0:T(8,128)(2,1)S(1)}, f32[2,1024,4096]{2,1,0:T(8,128)}, f32[2,4096,1024]{2,1,0:T(8,128)}, bf16[4,64,1024]{2,1,0:T(8,128)(2,1)S(1)}) conditional(s32[]{:T(128)} %convert_element_type.92, (f32[2,1024,4096]{2,1,0:T(8,128)}, f32[2,4096,1024]{2,1,0:T(8,128)}, bf16[4,64,1024]{2,1,0:T(8,128)(2,1)S(1)}) %tuple.177, ...), branch_computations={%region_6.6_spmd, %region_7.7_spmd.clone} | conditional | flops 2163802112 | bytes 156238368 | solution.py:106
  696.6 6.4 fusion.18
  709.1 6.6 constant_dynamic-slice_fusion.1
  715.7 8.5 bitcast_dynamic-update-slice_fusion.1
  724.3 6.6 constant_dynamic-slice_fusion
  730.8 9.8 bitcast_dynamic-update-slice_fusion
  744.8 39.0 %all-reduce.7.cloned.1.call-done = (bf16[4,64,1024]{2,1,0:T(8,128)(2,1)}, bf16[4,64,1024]{2,1,0:T(8,128)(2,1)}) async-done(((bf16[4,64,1024]{2,1,0:T(8,128)(2,1)}, bf16[4,64,1024]{2,1,0:T(8,128)(2,1)}), (bf16[4,64,1024]{2,1,0:T(8,128)(2,1)}, bf16[4,64,1024]{2,1,0:T(8,128)(2,1)})) %all-reduce.7.cloned.1.call-update) | async-done | bytes 1048592 | tf_op jit(solution)/shard_map/psum | solution.py:111
  783.7 2185.0 %all-reduce.5.cloned.1.call-done = (f32[2,1,1024,4096]{3,2,1,0:T(8,128)}, f32[2,1,4096,1024]{3,2,1,0:T(8,128)}) async-done(((f32[2,1,1024,4096]{3,2,1,0:T(8,128)}, f32[2,1,4096,1024]{3,2,1,0:T(8,128)}), (f32[2,1,1024,4096]{3,2,1,0:T(8,128)}, f32[2,1,4096,1024]{3,2,1,0:T(8,128)})) %all-reduce.5.cloned.1.call-update) | async-done | bytes 67108880 | tf_op jit(solution)/shard_map/psum | solution.py:113
  2972.6 26.6 copy.66
  3003.3 11.7 copy.67
  (135 shorter events, 282.6 us)
Async XLA Ops:
  7.2 776.5 %all-reduce.7.cloned.1.call-start = ((), (), s32[]{:S(2)}) async-start(), calls=%async_computation.1 | async-start | bytes 2097152 | tf_op jit(solution)/shard_map/psum | solution.py:111
  23.6 4.4 collective-permute-start
  40.0 4.4 collective-permute-start
  56.4 4.4 collective-permute-start
  72.7 4.4 collective-permute-start
  89.1 4.4 collective-permute-start
  105.5 4.4 collective-permute-start
  121.8 4.4 collective-permute-start
  138.3 4.4 collective-permute-start
  142.8 13.9 collective-permute-start
  156.7 13.9 collective-permute-start
  170.6 14.0 collective-permute-start
  208.4 46.8 %collective-permute-start.1 = (bf16[64,1024]{1,0:T(8,128)(2,1)S(1)}, bf16[64,1024]{1,0:T(8,128)(2,1)S(1)}, u32[]{:S(2)}, u32[]{:S(2)}) collective-permute-start(bf16[64,1024]{1,0:T(8,128)(2,1)S(1)} %get-tuple-element.1699), channel_id=1, source_target_pairs={{0,3},{1,0},{2,1},{3,2},{4,7},{5,4},{6,5},{7,6},{8,11},{9,8},{10,9... | collective-permute-start | bytes 393224 | tf_op jit(solution)/shard_map/while/body/eval_jaxpr/ppermute | solution.py:107
  255.2 49.3 %collective-permute-start.1 = (bf16[64,1024]{1,0:T(8,128)(2,1)S(1)}, bf16[64,1024]{1,0:T(8,128)(2,1)S(1)}, u32[]{:S(2)}, u32[]{:S(2)}) collective-permute-start(bf16[64,1024]{1,0:T(8,128)(2,1)S(1)} %get-tuple-element.1699), channel_id=1, source_target_pairs={{0,3},{1,0},{2,1},{3,2},{4,7},{5,4},{6,5},{7,6},{8,11},{9,8},{10,9... | collective-permute-start | bytes 393224 | tf_op jit(solution)/shard_map/while/body/eval_jaxpr/ppermute | solution.py:107
  304.6 49.3 %collective-permute-start.1 = (bf16[64,1024]{1,0:T(8,128)(2,1)S(1)}, bf16[64,1024]{1,0:T(8,128)(2,1)S(1)}, u32[]{:S(2)}, u32[]{:S(2)}) collective-permute-start(bf16[64,1024]{1,0:T(8,128)(2,1)S(1)} %get-tuple-element.1699), channel_id=1, source_target_pairs={{0,3},{1,0},{2,1},{3,2},{4,7},{5,4},{6,5},{7,6},{8,11},{9,8},{10,9... | collective-permute-start | bytes 393224 | tf_op jit(solution)/shard_map/while/body/eval_jaxpr/ppermute | solution.py:107
  398.9 4.4 collective-permute-start.1
  448.2 4.4 collective-permute-start.1
  497.6 4.4 collective-permute-start.1
  546.9 4.4 collective-permute-start.1
  596.3 4.4 collective-permute-start.1
  645.6 2.5 collective-permute-start.1
  693.1 2.5 collective-permute-start.1
  740.6 2.5 collective-permute-start.1
  744.0 2224.7 %all-reduce.5.cloned.1.call-start = ((), (), s32[]{:S(2)}) async-start(), calls=%async_computation | async-start | bytes 134217728 | tf_op jit(solution)/shard_map/psum | solution.py:113
  2970.5 28.7 slice-start
  2972.6 26.7 slice-start.1
  2972.6 26.7 slice-start.2
  2972.6 26.7 slice-start.3
  2972.6 26.7 slice-start.4
  2972.6 28.3 slice-start.5
  2972.6 29.5 slice-start.6
  2972.6 30.7 %slice-start.7 = ((s8[33554432]{0:T(1024)(128)(4,1)}), s8[4194304]{0:T(1024)(128)(4,1)S(1)}, s32[]{:S(2)}) async-start(s8[33554432]{0:T(1024)(128)(4,1)} %bitcast.102), calls=%async_computation.9 | async-start | bytes 8388608
Sparse Core Ops, SparseCore 0:
  744.1 39.5 all-reduce.6
  786.9 2181.6 all-reduce.4
where the time goes:
time: 3020 us
  waiting for transfers between devices  2320 us (77%)
  matrix products  334 us (11%)
  local copies, waits for them, and re-layouts  179 us (6%)
  starting transfers between devices  157 us (5%)
    psum x1, waiting for transfers between devices, local_fn(): grad_first = lax.psum(acc_first, 'data')  2180 us
    ppermute x11, starting transfers between devices, bwd_tick(): lax.ppermute(g_prev, 'stage', to_prev)  147 us
    dynamic_slice x24, local copies, waits for them, and re-layouts, pick_row(): return lax.dynamic_index_in_dim(stacked, row_idx, 0, keepdims=False)  105 us
    dot_general x8, matrix products, layer_backward(): jnp.einsum('tf,td->fd', hidden, g_next, preferred_element_type=jnp.float32)  78.3 us
    dot_general x8, matrix products, layer_backward(): jnp.einsum('td,tf->df', h_in, grad_pre, preferred_element_type=jnp.float32)  68.3 us
    ppermute x11, waiting for transfers between devices, fwd_tick(): return (lax.ppermute(h_out, 'stage', to_next), h_saved, pre_saved, y_buf)  67.6 us
  transfers between devices with their start and end apart: 24, of which 24 were waited for; matrix products, arithmetic and copies ran while one was open for 0% of the time, Pallas kernels for 0%

commit v1 on v0

v1 whole, which is shorter than its diff:
```python
import functools
import math
import jax
import jax.numpy as jnp
from jax import lax
from jax.experimental import pallas as pl
from jax.experimental.pallas import tpu as pltpu
from jax.sharding import PartitionSpec as P

MESH = pl.DeviceIdType.MESH
VMEM_BYTES = 67_000_000
BLOCK_OF = (0, 1, 3, 2)
GELU_K0 = math.sqrt(2.0 / math.pi)
GELU_K1 = GELU_K0 * 0.044715


def gelu_pair(z):
    sq = z * z
    cdf = 0.5 * jnp.tanh(z * (GELU_K0 + GELU_K1 * sq)) + 0.5
    val = z * cdf
    slope = cdf + (val * (1.0 - cdf)) * (2.0 * GELU_K0 + 6.0 * GELU_K1 * sq)
    return val, slope


def chain_kernel(stages, replicas, f_chunk,
                 x_ref, g_ref, w_in_ref, w_out_ref,
                 y_ref, dx_ref, h_out, e_out, a_out, q_out, slope_hbm,
                 h_buf, e_buf, win, wout, slope_buf, a_buf, q_buf, f_send_buf, b_send_buf,
                 w_sem, f_recv, b_recv, f_send, b_send, x_send, g_send,
                 slope_wr, slope_rd, a_wr, q_wr, h_wr, e_wr,
                 y_send, y_loc, y_recv, d_send, d_loc, d_recv):
    stage = lax.axis_index('stage')
    data = lax.axis_index('data')
    rows = x_ref.shape[0]
    fu, bu = rows // 2, rows
    f_per, b_per = 2 * replicas, replicas
    f_units, b_units = 2 * f_per, 2 * b_per
    hidden = win.shape[2]
    is_first = stage == 0
    is_last = stage == stages - 1
    nxt = lax.rem(stage + 1, stages)
    prv = lax.rem(stage + stages - 1, stages)

    def weight_copy(layer, which):
        src, dst = ((w_in_ref, win), (w_out_ref, wout))[which]
        return pltpu.make_async_copy(src.at[layer, 0], dst.at[layer], w_sem.at[layer, which])

    for layer in range(2):
        for which in range(2):
            weight_copy(layer, which).start()

    barrier = pltpu.get_barrier_semaphore()
    for off in range(1, stages):
        pl.semaphore_signal(barrier, inc=1, device_id={'stage': lax.rem(stage + off, stages)}, device_id_type=MESH)
    for off in range(1, replicas):
        pl.semaphore_signal(barrier, inc=1, device_id={'data': lax.rem(data + off, replicas)}, device_id_type=MESH)
    pl.semaphore_wait(barrier, stages + replicas - 2)

    def x_copy(blk, half):
        slot = 2 * blk + half
        return pltpu.make_async_remote_copy(
            src_ref=x_ref.at[pl.ds(half * fu, fu)], dst_ref=h_buf.at[0, pl.ds(slot * fu, fu)],
            send_sem=x_send.at[slot], recv_sem=f_recv.at[slot],
            device_id={'data': lax.rem(data + replicas - BLOCK_OF[blk], replicas)}, device_id_type=MESH)

    def g_copy(blk):
        return pltpu.make_async_remote_copy(
            src_ref=g_ref, dst_ref=e_buf.at[1, pl.ds(blk * bu, bu)],
            send_sem=g_send.at[blk], recv_sem=b_recv.at[blk],
            device_id={'data': lax.rem(data + replicas - BLOCK_OF[blk], replicas)}, device_id_type=MESH)

    @pl.when(is_first)
    def _():
        for half in range(2):
            pltpu.make_async_copy(x_ref.at[pl.ds(half * fu, fu)], h_buf.at[0, pl.ds(half * fu, fu)], f_recv.at[half]).start()
        for blk in range(1, replicas):
            for half in range(2):
                x_copy(blk, half).start()

    @pl.when(is_last)
    def _():
        pltpu.make_async_copy(g_ref, e_buf.at[1, pl.ds(0, bu)], b_recv.at[0]).start()
        for blk in range(1, replicas):
            g_copy(blk).start()

    def f_hop(n):
        v, i = n // f_per, lax.rem(n, f_per)
        slot = lax.rem(n, 2)
        return pltpu.make_async_remote_copy(
            src_ref=f_send_buf.at[slot], dst_ref=h_buf.at[lax.rem(v + is_last.astype(jnp.int32), 2), pl.ds(pl.multiple_of(i * fu, fu), fu)],
            send_sem=f_send.at[slot], recv_sem=f_recv.at[lax.rem(n + f_per * is_last.astype(jnp.int32), f_units)],
            device_id={'stage': nxt}, device_id_type=MESH)

    def y_copies(i):
        src = f_send_buf.at[i]
        dst = y_ref.at[pl.ds(i * fu, fu)]
        remote = [pltpu.make_async_remote_copy(
            src_ref=src, dst_ref=dst, send_sem=y_send.at[i, k], recv_sem=y_recv.at[i],
            device_id={'stage': k}, device_id_type=MESH) for k in range(stages - 1)]
        return remote, pltpu.make_async_copy(src, dst, y_loc.at[i])

    def slope_write(n):
        v, i = n // f_per, lax.rem(n, f_per)
        slot = lax.rem(n, 2)
        return pltpu.make_async_copy(
            slope_buf.at[pl.ds(pl.multiple_of(bu + slot * fu, fu), fu)],
            slope_hbm.at[v, pl.ds(pl.multiple_of(i * fu, fu), fu)], slope_wr.at[slot])

    def a_write(n):
        v, i = n // f_per, lax.rem(n, f_per)
        slot = lax.rem(n, 2)
        return pltpu.make_async_copy(a_buf.at[slot], a_out.at[v, pl.ds(pl.multiple_of(i * fu, fu), fu)], a_wr.at[slot])

    def hops(n):
        return jnp.logical_not(jnp.logical_and(is_last, n >= f_per))

    def f_step(n, carry):
        v, i = n // f_per, lax.rem(n, f_per)
        slot = lax.rem(n, 2)
        row0 = pl.multiple_of(i * fu, fu)

        @pl.when(i == 0)
        def _():
            pltpu.make_async_copy(w_in_ref.at[v, 0], win.at[v], w_sem.at[v, 0]).wait()
            pltpu.make_async_copy(w_out_ref.at[v, 0], wout.at[v], w_sem.at[v, 1]).wait()

        @pl.when(n >= 2)
        def _():
            slope_write(n - 2).wait()
            a_write(n - 2).wait()

        pltpu.make_async_copy(x_ref.at[pl.ds(0, fu)], h_buf.at[v, pl.ds(row0, fu)], f_recv.at[n]).wait()
        h_in = h_buf[v, pl.ds(row0, fu), :]
        for c in range(hidden // f_chunk):
            cols = pl.ds(c * f_chunk, f_chunk)
            z = jnp.dot(h_in, win[v, :, cols], preferred_element_type=jnp.float32)
            val, slope = gelu_pair(z)
            slope_buf[pl.ds(pl.multiple_of(bu + slot * fu, fu), fu), cols] = slope
            a_buf[slot, :, cols] = val.astype(jnp.bfloat16)
        slope_write(n).start()
        a_write(n).start()

        @pl.when(jnp.logical_and(n >= 2, hops(n - 2)))
        def _():
            f_hop(n - 2).wait_send()

        @pl.when(jnp.logical_or(hops(n), i < 2))
        def _():
            delta = jnp.dot(a_buf[slot], wout[v], preferred_element_type=jnp.float32)
            f_send_buf[slot] = (h_buf[v, pl.ds(row0, fu), :].astype(jnp.float32) + delta).astype(jnp.bfloat16)

        @pl.when(hops(n))
        def _():
            f_hop(n).start()

        for k in range(2):
            @pl.when(jnp.logical_and(is_last, n == f_per + k))
            def _():
                remote, local = y_copies(k)
                for copy in remote:
                    copy.start()
                local.start()
        return carry

    lax.fori_loop(0, f_units, f_step, 0)
    for k in range(2):
        n = f_units - 2 + k
        slope_write(n).wait()
        a_write(n).wait()

    @pl.when(jnp.logical_not(is_last))
    def _():
        for k in range(2):
            f_hop(f_units - 2 + k).wait_send()

    def h_copy(layer):
        return pltpu.make_async_copy(h_buf.at[layer], h_out.at[layer], h_wr.at[layer])

    def e_copy(layer):
        return pltpu.make_async_copy(e_buf.at[layer], e_out.at[layer], e_wr.at[layer])

    for layer in range(2):
        h_copy(layer).start()

    def slope_read(n):
        v, j = 1 - n // b_per, lax.rem(n, b_per)
        slot = lax.rem(n, 2)
        return pltpu.make_async_copy(
            slope_hbm.at[v, pl.ds(pl.multiple_of(j * bu, bu), bu)],
            slope_buf.at[pl.ds(pl.multiple_of(slot * bu, bu), bu)], slope_rd.at[slot])

    def q_write(n):
        v, j = 1 - n // b_per, lax.rem(n, b_per)
        slot = lax.rem(n, 2)
        return pltpu.make_async_copy(q_buf.at[slot], q_out.at[v, pl.ds(pl.multiple_of(j * bu, bu), bu)], q_wr.at[slot])

    def b_hop(n):
        v, j = 1 - n // b_per, lax.rem(n, b_per)
        slot = lax.rem(n, 2)
        wrap = is_first.astype(jnp.int32)
        return pltpu.make_async_remote_copy(
            src_ref=b_send_buf.at[slot], dst_ref=e_buf.at[lax.rem(v + wrap, 2), pl.ds(pl.multiple_of(j * bu, bu), bu)],
            send_sem=b_send.at[slot], recv_sem=b_recv.at[lax.rem(n + b_per * wrap, b_units)],
            device_id={'stage': prv}, device_id_type=MESH)

    def d_copies():
        src = b_send_buf.at[0]
        remote = [pltpu.make_async_remote_copy(
            src_ref=src, dst_ref=dx_ref, send_sem=d_send.at[k - 1], recv_sem=d_recv.at[0],
            device_id={'stage': k}, device_id_type=MESH) for k in range(1, stages)]
        return remote, pltpu.make_async_copy(src, dx_ref, d_loc.at[0])

    def b_hops(n):
        return jnp.logical_not(jnp.logical_and(is_first, n >= b_per))

    for n in range(2):
        slope_read(n).start()

    def b_step(n, carry):
        v, j = 1 - n // b_per, lax.rem(n, b_per)
        slot = lax.rem(n, 2)
        row0 = pl.multiple_of(j * bu, bu)
        slope_read(n).wait()

        @pl.when(n >= 2)
        def _():
            q_write(n - 2).wait()

        pltpu.make_async_copy(g_ref, e_buf.at[v, pl.ds(row0, bu)], b_recv.at[n]).wait()
        e_in = e_buf[v, pl.ds(row0, bu), :]
        for c in range(hidden // f_chunk):
            cols = pl.ds(c * f_chunk, f_chunk)
            d_act = lax.dot_general(e_in, wout[v, cols, :], (((1,), (1,)), ((), ())), preferred_element_type=jnp.float32)
            slope = slope_buf[pl.ds(pl.multiple_of(slot * bu, bu), bu), cols]
            q_buf[slot, :, cols] = (slope * d_act).astype(jnp.bfloat16)
        q_write(n).start()

        @pl.when(n + 2 < b_units)
        def _():
            slope_read(n + 2).start()

        @pl.when(jnp.logical_and(n >= 2, b_hops(n - 2)))
        def _():
            b_hop(n - 2).wait_send()

        @pl.when(jnp.logical_or(b_hops(n), j == 0))
        def _():
            delta = lax.dot_general(q_buf[slot], win[v], (((1,), (1,)), ((), ())), preferred_element_type=jnp.float32)
            b_send_buf[slot] = (e_buf[v, pl.ds(row0, bu), :].astype(jnp.float32) + delta).astype(jnp.bfloat16)

        @pl.when(b_hops(n))
        def _():
            b_hop(n).start()

        @pl.when(jnp.logical_and(is_first, n == b_per))
        def _():
            remote, local = d_copies()
            for copy in remote:
                copy.start()
            local.start()
        return carry

    @pl.when(is_last)
    def _():
        for k in range(2):
            remote, local = y_copies(k)
            for copy in remote:
                copy.wait_send()
            local.wait()

    lax.fori_loop(0, b_units, b_step, 0)
    for layer in range(2):
        e_copy(layer).start()
    for k in range(2):
        q_write(b_units - 2 + k).wait()

    @pl.when(jnp.logical_not(is_first))
    def _():
        for k in range(2):
            b_hop(b_units - 2 + k).wait_send()
        pltpu.make_async_copy(b_send_buf.at[0], dx_ref, d_recv.at[0]).wait()

    @pl.when(is_first)
    def _():
        remote, local = d_copies()
        for copy in remote:
            copy.wait_send()
        local.wait()
        for blk in range(1, replicas):
            for half in range(2):
                x_copy(blk, half).wait_send()

    @pl.when(jnp.logical_not(is_last))
    def _():
        for k in range(2):
            pltpu.make_async_copy(f_send_buf.at[k], y_ref.at[pl.ds(k * fu, fu)], y_recv.at[k]).wait()

    @pl.when(is_last)
    def _():
        for blk in range(1, replicas):
            g_copy(blk).wait_send()

    for layer in range(2):
        h_copy(layer).wait()
        e_copy(layer).wait()


def run_chain(x, g, w_in, w_out, stages, replicas):
    rows, model = x.shape
    hidden = w_in.shape[-1]
    total = rows * replicas
    fu, bu = rows // 2, rows
    f_chunk = hidden // 4
    any_spec = pl.BlockSpec(memory_space=pl.ANY)
    bf, f32 = jnp.bfloat16, jnp.float32
    dma = pltpu.SemaphoreType.DMA
    shape = jax.ShapeDtypeStruct
    f_units, b_units = 4 * replicas, 2 * replicas
    return pl.pallas_call(
        functools.partial(chain_kernel, stages, replicas, f_chunk),
        out_shape=(shape((rows, model), bf), shape((rows, model), bf),
                   shape((2, total, model), bf), shape((2, total, model), bf),
                   shape((2, total, hidden), bf), shape((2, total, hidden), bf),
                   shape((2, total, hidden), f32)),
        in_specs=[any_spec] * 4,
        out_specs=(any_spec,) * 7,
        scratch_shapes=[
            pltpu.VMEM((2, total, model), bf), pltpu.VMEM((2, total, model), bf),
            pltpu.VMEM((2, model, hidden), bf), pltpu.VMEM((2, hidden, model), bf),
            pltpu.VMEM((2 * bu, hidden), f32), pltpu.VMEM((2, fu, hidden), bf), pltpu.VMEM((2, bu, hidden), bf),
            pltpu.VMEM((2, fu, model), bf), pltpu.VMEM((2, bu, model), bf),
            dma((2, 2)), dma((f_units,)), dma((b_units,)), dma((2,)), dma((2,)), dma((2 * replicas,)), dma((replicas,)),
            dma((2,)), dma((2,)), dma((2,)), dma((2,)), dma((2,)), dma((2,)),
            dma((2, stages - 1)), dma((2,)), dma((2,)), dma((stages - 1,)), dma((1,)), dma((1,)),
        ],
        compiler_params=pltpu.CompilerParams(collective_id=0, has_side_effects=True, vmem_limit_bytes=VMEM_BYTES),
        name='chain',
    )(x, g, w_in, w_out)


def solution(mesh):
    stages = mesh.shape['stage']
    replicas = mesh.shape['data']

    def local_fn(x, g, w_in, w_out):
        micro, tokens, model = x.shape
        y, dx, h_all, e_all, a_all, q_all, _ = run_chain(
            x.reshape(micro * tokens, model), g.reshape(micro * tokens, model), w_in, w_out, stages, replicas)
        grad_first = jnp.einsum('vtd,vtf->vdf', h_all, q_all, preferred_element_type=jnp.float32)
        grad_second = jnp.einsum('vtf,vtd->vfd', a_all, e_all, preferred_element_type=jnp.float32)
        return y.reshape(x.shape), dx.reshape(x.shape), grad_first[:, None], grad_second[:, None]

    spec_rows = P(('part', 'data'))
    spec_weights = P(None, 'stage')
    spec_grads = P('part', 'stage')
    return jax.shard_map(local_fn, mesh=mesh, in_specs=(spec_rows, spec_rows, spec_weights, spec_weights), out_specs=(spec_rows, spec_rows, spec_grads, spec_grads), check_vma=False)
```

time: 3020 us -> 231 us (0.08)
  waiting for transfers between devices: 2320 us -> 0 us
  matrix products: 334 us -> 55.3 us
  local copies, waits for them, and re-layouts: 179 us -> 1.59 us
  Pallas kernels: 0 us -> 173 us
  starting transfers between devices: 157 us -> 0 us
    psum x2 -> x0, waiting for transfers between devices: 2220 us -> none  [the longest x1 2180 us: local_fn(): grad_first = lax.psum(acc_first, 'data')]
    dot_general x48 -> x2, matrix products: 334 us -> 55.3 us  [the longest x1 28.2 us: local_fn(): jnp.einsum('vtd,vtf->vdf', h_all, q_all, preferred_element_type=jnp.float32)]
    pallas_call x0 -> x1, Pallas kernels: none -> 173 us  [run_chain(): pl.pallas_call(functools.partial(chain_kernel, stages, replicas, f_chunk)...]
    ppermute x22 -> x0, starting transfers between devices: 157 us -> none  [the longest x11 147 us: bwd_tick(): lax.ppermute(g_prev, 'stage', to_prev)]
    dynamic_slice x24 -> x0, local copies, waits for them, and re-layouts: 105 us -> none  [pick_row(): return lax.dynamic_index_in_dim(stacked, row_idx, 0, keepdims=False)]
    ppermute x22 -> x0, waiting for transfers between devices: 95.3 us -> none  [the longest x11 67.6 us: fwd_tick(): return (lax.ppermute(h_out, 'stage', to_next), h_saved, pre_saved, y_buf)]
    unnamed x20 -> x6, local copies, waits for them, and re-layouts: 46.2 us -> 1.59 us
  transfers between devices with their start and end apart: 24 -> 0, of which waited for: 24 -> 0; matrix products, arithmetic and copies ran while one was open for 0% -> 0% of each run, Pallas kernels for 0% -> 0%
where the time goes in v1:
time: 231 us
  Pallas kernels  173 us (75%)
  matrix products  55.3 us (24%)
    pallas_call x1, Pallas kernels, run_chain(): pl.pallas_call(functools.partial(chain_kernel, stages, replicas, f_chunk)...  173 us
    dot_general x1, matrix products, local_fn(): jnp.einsum('vtd,vtf->vdf', h_all, q_all, preferred_element_type=jnp.float32)  28.2 us
    dot_general x1, matrix products, local_fn(): jnp.einsum('vtf,vtd->vfd', a_all, e_all, preferred_element_type=jnp.float32)  27.1 us

profile of v1, /device:TPU:0, one launch (start us, length us, event | category | flops | bytes accessed | tf_op | source)
XLA Modules:
  0.0 230.5 jit_solution(7821400672538039287)
XLA Ops:
  0.6 173.0 %chain.1 = (bf16[256,1024]{1,0:T(8,128)(2,1)}, bf16[256,1024]{1,0:T(8,128)(2,1)}, bf16[2,1024,1024]{2,1,0:T(8,128)(2,1)}, bf16[2,1024,1024]{2,1,0:T(8,128)(2,1)}...) custom-call(bf16[256,1024]{1,0:T(8,128)(2,1)} %bitcast.16, ...), custom_call_target="tpu_custom_call" | custom-call | tf_op jit(solution)/shard_map/chain/pallas_call | solution.py:319
  173.6 28.2 %convolution_bitcast_fusion.1 = f32[2,1,1024,4096]{3,2,1,0:T(8,128)} fusion(bf16[2,1024,1024]{2,1,0:T(8,128)(2,1)} %get-tuple-element.12, bf16[2,1024,4096]{2,1,0:T(8,128)(2,1)} %get-tuple-element.13), kind=kOutput, calls=%fused_computation.1 | convolution fusion | flops 17179869184 | bytes 54525952 | tf_op jit(solution)/shard_map/vtd,vtf->vdf/dot_general | solution.py:349
  201.8 0.0 copy-start.1
  201.8 0.0 copy-start
  201.8 27.1 %convolution_bitcast_fusion = f32[2,1,4096,1024]{3,2,1,0:T(8,128)} fusion(bf16[2,1024,4096]{2,1,0:T(8,128)(2,1)} %get-tuple-element.14, bf16[2,1024,1024]{2,1,0:T(8,128)(2,1)} %get-tuple-element.15), kind=kOutput, calls=%fused_computation | convolution fusion | flops 17179869184 | bytes 54525952 | tf_op jit(solution)/shard_map/vtf,vtd->vfd/dot_general | solution.py:350
  228.9 0.0 copy-done.1
  228.9 0.8 copy.16
  229.7 0.0 copy-done
  229.7 0.8 copy.17
Async XLA Ops:
  201.8 27.1 %copy-start.1 = (bf16[256,1024]{1,0:T(8,128)(2,1)S(1)}, bf16[256,1024]{1,0:T(8,128)(2,1)}, u32[]{:S(2)}) copy-start(bf16[256,1024]{1,0:T(8,128)(2,1)} %get-tuple-element.10) | copy-start | bytes 1572868
  201.8 27.9 %copy-start = (bf16[256,1024]{1,0:T(8,128)(2,1)S(1)}, bf16[256,1024]{1,0:T(8,128)(2,1)}, u32[]{:S(2)}) copy-start(bf16[256,1024]{1,0:T(8,128)(2,1)} %get-tuple-element.11) | copy-start | bytes 1572868

commit v2 on v1

v2 whole, which is shorter than its diff:
```python
import functools
import math
import jax
import jax.numpy as jnp
from jax import lax
from jax.experimental import pallas as pl
from jax.experimental.pallas import tpu as pltpu
from jax.sharding import PartitionSpec as P

MESH = pl.DeviceIdType.MESH
VMEM_BYTES = 67_000_000
BLOCK_OF = (0, 1, 3, 2)
GELU_K0 = math.sqrt(2.0 / math.pi)
GELU_K1 = GELU_K0 * 0.044715


def gelu_pair(z):
    sq = z * z
    cdf = 0.5 * jnp.tanh(z * (GELU_K0 + GELU_K1 * sq)) + 0.5
    val = z * cdf
    slope = cdf + (val * (1.0 - cdf)) * (2.0 * GELU_K0 + 6.0 * GELU_K1 * sq)
    return val, slope


def chain_kernel(stages, replicas, f_chunk,
                 x_ref, g_ref, w_in_ref, w_out_ref,
                 y_ref, dx_ref, h_out, e_out, a_out, q_out, slope_hbm, wide_hbm, tall_hbm,
                 h_buf, e_buf, wide, tall, slope_buf, a_buf, q_buf, f_send_buf, b_send_buf, wide_stage, tall_stage,
                 w_sem, wt_wr, wt_rd, f_recv, b_recv, f_send, b_send, x_send, g_send,
                 slope_wr, slope_rd, a_wr, q_wr, h_wr, e_wr,
                 y_send, y_loc, y_recv, d_send, d_loc, d_recv):
    stage = lax.axis_index('stage')
    data = lax.axis_index('data')
    unit = x_ref.shape[0] // 2
    per = 2 * replicas
    hidden = wide.shape[2]
    part_f = hidden // per
    is_first = stage == 0
    is_last = stage == stages - 1
    nxt = lax.rem(stage + 1, stages)
    prv = lax.rem(stage + stages - 1, stages)

    def rows_of(i):
        return pl.ds(pl.multiple_of(i * unit, unit), unit)

    def weight_copies(layer):
        return (pltpu.make_async_copy(w_in_ref.at[layer, 0], wide.at[layer], w_sem.at[layer, 0]),
                pltpu.make_async_copy(w_out_ref.at[layer, 0], tall.at[layer], w_sem.at[layer, 1]))

    for layer in range(2):
        for copy in weight_copies(layer):
            copy.start()

    barrier = pltpu.get_barrier_semaphore()
    for off in range(1, stages):
        pl.semaphore_signal(barrier, inc=1, device_id={'stage': lax.rem(stage + off, stages)}, device_id_type=MESH)
    for off in range(1, replicas):
        pl.semaphore_signal(barrier, inc=1, device_id={'data': lax.rem(data + off, replicas)}, device_id_type=MESH)
    pl.semaphore_wait(barrier, stages + replicas - 2)

    def share_copy(src, dst, send_sem, recv_sem, blk, half):
        slot = 2 * blk + half
        return pltpu.make_async_remote_copy(
            src_ref=src.at[pl.ds(half * unit, unit)], dst_ref=dst.at[pl.ds(slot * unit, unit)],
            send_sem=send_sem.at[slot], recv_sem=recv_sem.at[slot],
            device_id={'data': lax.rem(data + replicas - BLOCK_OF[blk], replicas)}, device_id_type=MESH)

    def share(src, dst, send_sem, recv_sem):
        for half in range(2):
            rows = pl.ds(half * unit, unit)
            pltpu.make_async_copy(src.at[rows], dst.at[rows], recv_sem.at[half]).start()
        for blk in range(1, replicas):
            for half in range(2):
                share_copy(src, dst, send_sem, recv_sem, blk, half).start()

    @pl.when(is_first)
    def _():
        share(x_ref, h_buf.at[0], x_send, f_recv)

    @pl.when(is_last)
    def _():
        share(g_ref, e_buf.at[1], g_send, b_recv)

    def f_hop(v, i):
        slot = lax.rem(i, 2)
        last = is_last.astype(jnp.int32)
        return pltpu.make_async_remote_copy(
            src_ref=f_send_buf.at[slot], dst_ref=h_buf.at[lax.rem(v + last, 2), rows_of(i)],
            send_sem=f_send.at[slot], recv_sem=f_recv.at[lax.rem(v * per + i + per * last, 2 * per)],
            device_id={'stage': nxt}, device_id_type=MESH)

    def y_copies(i):
        src = f_send_buf.at[i]
        dst = y_ref.at[pl.ds(i * unit, unit)]
        remote = [pltpu.make_async_remote_copy(
            src_ref=src, dst_ref=dst, send_sem=y_send.at[i, k], recv_sem=y_recv.at[i],
            device_id={'stage': k}, device_id_type=MESH) for k in range(stages - 1)]
        return remote, pltpu.make_async_copy(src, dst, y_loc.at[i])

    def f_writes(v, i):
        slot = lax.rem(i, 2)
        return (pltpu.make_async_copy(slope_buf.at[rows_of(2 + slot)], slope_hbm.at[v, rows_of(i)], slope_wr.at[slot]),
                pltpu.make_async_copy(a_buf.at[slot], a_out.at[v, rows_of(i)], a_wr.at[slot]))

    def wt_writes(i):
        slot = lax.rem(i, 2)
        return (pltpu.make_async_copy(wide_stage.at[slot], wide_hbm.at[:, pl.ds(pl.multiple_of(i * part_f, part_f), part_f)], wt_wr.at[slot, 0]),
                pltpu.make_async_copy(tall_stage.at[slot], tall_hbm.at[pl.ds(pl.multiple_of(i * part_f, part_f), part_f)], wt_wr.at[slot, 1]))

    def f_compute(v, i, full):
        slot = lax.rem(i, 2)
        h_in = h_buf[v, rows_of(i), :]
        for c in range(hidden // f_chunk):
            cols = pl.ds(c * f_chunk, f_chunk)
            z = jnp.dot(h_in, wide[v, :, cols], preferred_element_type=jnp.float32)
            val, slope = gelu_pair(z)
            slope_buf[rows_of(2 + slot), cols] = slope
            a_buf[slot, :, cols] = val.astype(jnp.bfloat16)
        strip = pl.ds(pl.multiple_of(i * part_f, part_f), part_f)
        if v == 0:
            wide_stage[slot] = tall[v, strip, :].T
            tall_stage[slot] = wide[v, :, strip].T
        else:
            wide[0, :, strip] = tall[v, strip, :].T
            tall[0, strip, :] = wide[v, :, strip].T
        if full:
            delta = jnp.dot(a_buf[slot], tall[v], preferred_element_type=jnp.float32)
            f_send_buf[slot] = (h_in.astype(jnp.float32) + delta).astype(jnp.bfloat16)

    def f_wait(v, i):
        pltpu.make_async_copy(x_ref.at[pl.ds(0, unit)], h_buf.at[v, rows_of(i)], f_recv.at[v * per + i]).wait()

    for copy in weight_copies(0):
        copy.wait()

    def f_step_0(i, carry):
        @pl.when(i >= 2)
        def _():
            for copy in f_writes(0, i - 2) + wt_writes(i - 2):
                copy.wait()
            f_hop(0, i - 2).wait_send()

        f_wait(0, i)
        f_compute(0, i, True)
        f_hop(0, i).start()
        for copy in f_writes(0, i) + wt_writes(i):
            copy.start()
        return carry

    lax.fori_loop(0, per, f_step_0, 0)
    for copy in weight_copies(1):
        copy.wait()
    for i in range(per - 2, per):
        f_hop(0, i).wait_send()

    def slope_read(v, j):
        slot = lax.rem(j, 2)
        return pltpu.make_async_copy(slope_hbm.at[v, rows_of(j)], slope_buf.at[rows_of(slot)], slope_rd.at[slot])

    def f_step_1(i, carry):
        @pl.when(i < 2)
        def _():
            for copy in f_writes(0, per - 2 + i) + wt_writes(per - 2 + i):
                copy.wait()

        @pl.when(i >= 2)
        def _():
            for copy in f_writes(1, i - 2):
                copy.wait()

        for j in range(2):
            @pl.when(i == 2 + j)
            def _():
                slope_read(1, j).start()

        @pl.when(jnp.logical_and(i >= 2, jnp.logical_not(is_last)))
        def _():
            f_hop(1, i - 2).wait_send()

        f_wait(1, i)

        @pl.when(jnp.logical_or(jnp.logical_not(is_last), i < 2))
        def _():
            f_compute(1, i, True)

        @pl.when(jnp.logical_and(is_last, i >= 2))
        def _():
            f_compute(1, i, False)

        @pl.when(jnp.logical_not(is_last))
        def _():
            f_hop(1, i).start()

        for copy in f_writes(1, i):
            copy.start()
        for k in range(2):
            @pl.when(jnp.logical_and(is_last, i == k))
            def _():
                remote, local = y_copies(k)
                for copy in remote:
                    copy.start()
                local.start()
        return carry

    lax.fori_loop(0, per, f_step_1, 0)

    def wt_reads():
        return (pltpu.make_async_copy(wide_hbm, wide.at[1], wt_rd.at[0]),
                pltpu.make_async_copy(tall_hbm, tall.at[1], wt_rd.at[1]))

    def h_copy(layer):
        return pltpu.make_async_copy(h_buf.at[layer], h_out.at[layer], h_wr.at[layer])

    def e_copy(layer):
        return pltpu.make_async_copy(e_buf.at[layer], e_out.at[layer], e_wr.at[layer])

    def q_write(v, j):
        slot = lax.rem(j, 2)
        return pltpu.make_async_copy(q_buf.at[slot], q_out.at[v, rows_of(j)], q_wr.at[slot])

    def b_hop(v, j):
        slot = lax.rem(j, 2)
        wrap = is_first.astype(jnp.int32)
        return pltpu.make_async_remote_copy(
            src_ref=b_send_buf.at[slot], dst_ref=e_buf.at[lax.rem(v + wrap, 2), rows_of(j)],
            send_sem=b_send.at[slot], recv_sem=b_recv.at[lax.rem((1 - v) * per + j + per * wrap, 2 * per)],
            device_id={'stage': prv}, device_id_type=MESH)

    def d_copies(i):
        src = b_send_buf.at[i]
        dst = dx_ref.at[pl.ds(i * unit, unit)]
        remote = [pltpu.make_async_remote_copy(
            src_ref=src, dst_ref=dst, send_sem=d_send.at[i, k - 1], recv_sem=d_recv.at[i],
            device_id={'stage': k}, device_id_type=MESH) for k in range(1, stages)]
        return remote, pltpu.make_async_copy(src, dst, d_loc.at[i])

    def hops(v):
        return jnp.logical_not(jnp.logical_and(is_first, v == 0))

    for copy in wt_reads():
        copy.start()

    def b_compute(v, j, full):
        slot = lax.rem(j, 2)
        e_in = e_buf[v, rows_of(j), :]
        for c in range(hidden // f_chunk):
            cols = pl.ds(c * f_chunk, f_chunk)
            d_act = jnp.dot(e_in, wide[1 - v, :, cols], preferred_element_type=jnp.float32)
            q_buf[slot, :, cols] = (slope_buf[rows_of(slot), cols] * d_act).astype(jnp.bfloat16)
        if full:
            delta = jnp.dot(q_buf[slot], tall[1 - v], preferred_element_type=jnp.float32)
            b_send_buf[slot] = (e_in.astype(jnp.float32) + delta).astype(jnp.bfloat16)

    def b_step(n, carry):
        v, j = 1 - n // per, lax.rem(n, per)
        slope_read(v, j).wait()

        @pl.when(n == 1)
        def _():
            for i in range(per - 2, per):
                for copy in f_writes(1, i):
                    copy.wait()
            for layer in range(2):
                h_copy(layer).start()

        @pl.when(n == per)
        def _():
            for copy in wt_reads():
                copy.wait()
            e_copy(1).start()

        @pl.when(n >= 2)
        def _():
            back = n - 2
            q_write(1 - back // per, lax.rem(back, per)).wait()

        @pl.when(jnp.logical_and(n >= 2, hops(1 - (n - 2) // per)))
        def _():
            b_hop(1 - (n - 2) // per, lax.rem(n - 2, per)).wait_send()

        pltpu.make_async_copy(x_ref.at[pl.ds(0, unit)], e_buf.at[v, rows_of(j)], b_recv.at[n]).wait()

        @pl.when(jnp.logical_or(hops(v), j < 2))
        def _():
            b_compute(v, j, True)

        @pl.when(jnp.logical_not(jnp.logical_or(hops(v), j < 2)))
        def _():
            b_compute(v, j, False)

        @pl.when(hops(v))
        def _():
            b_hop(v, j).start()

        q_write(v, j).start()

        @pl.when(n + 2 < 2 * per)
        def _():
            ahead = n + 2
            slope_read(1 - ahead // per, lax.rem(ahead, per)).start()

        for k in range(2):
            @pl.when(jnp.logical_and(is_first, n == per + k))
            def _():
                remote, local = d_copies(k)
                for copy in remote:
                    copy.start()
                local.start()
        return carry

    lax.fori_loop(0, 2 * per, b_step, 0)
    e_copy(0).start()
    for j in range(per - 2, per):
        q_write(0, j).wait()

    def share_done(src, dst, send_sem, recv_sem):
        for blk in range(1, replicas):
            for half in range(2):
                share_copy(src, dst, send_sem, recv_sem, blk, half).wait_send()

    @pl.when(is_first)
    def _():
        for k in range(2):
            remote, local = d_copies(k)
            for copy in remote:
                copy.wait_send()
            local.wait()
        share_done(x_ref, h_buf.at[0], x_send, f_recv)

    @pl.when(jnp.logical_not(is_first))
    def _():
        for j in range(per - 2, per):
            b_hop(0, j).wait_send()
        for k in range(2):
            pltpu.make_async_copy(b_send_buf.at[k], dx_ref.at[pl.ds(k * unit, unit)], d_recv.at[k]).wait()

    @pl.when(is_last)
    def _():
        for k in range(2):
            remote, local = y_copies(k)
            for copy in remote:
                copy.wait_send()
            local.wait()
        share_done(g_ref, e_buf.at[1], g_send, b_recv)

    @pl.when(jnp.logical_not(is_last))
    def _():
        for i in range(per - 2, per):
            f_hop(1, i).wait_send()
        for k in range(2):
            pltpu.make_async_copy(f_send_buf.at[k], y_ref.at[pl.ds(k * unit, unit)], y_recv.at[k]).wait()

    for layer in range(2):
        h_copy(layer).wait()
        e_copy(layer).wait()


def run_chain(x, g, w_in, w_out, stages, replicas):
    rows, model = x.shape
    hidden = w_in.shape[-1]
    total = rows * replicas
    unit, per = rows // 2, 2 * replicas
    f_chunk = hidden // 4
    part_f = hidden // per
    any_spec = pl.BlockSpec(memory_space=pl.ANY)
    bf, f32 = jnp.bfloat16, jnp.float32
    dma = pltpu.SemaphoreType.DMA
    shape = jax.ShapeDtypeStruct
    return pl.pallas_call(
        functools.partial(chain_kernel, stages, replicas, f_chunk),
        out_shape=(shape((rows, model), bf), shape((rows, model), bf),
                   shape((2, total, model), bf), shape((2, total, model), bf),
                   shape((2, total, hidden), bf), shape((2, total, hidden), bf),
                   shape((2, total, hidden), f32), shape((model, hidden), bf), shape((hidden, model), bf)),
        in_specs=[any_spec] * 4,
        out_specs=(any_spec,) * 9,
        scratch_shapes=[
            pltpu.VMEM((2, total, model), bf), pltpu.VMEM((2, total, model), bf),
            pltpu.VMEM((2, model, hidden), bf), pltpu.VMEM((2, hidden, model), bf),
            pltpu.VMEM((4 * unit, hidden), f32), pltpu.VMEM((2, unit, hidden), bf), pltpu.VMEM((2, unit, hidden), bf),
            pltpu.VMEM((2, unit, model), bf), pltpu.VMEM((2, unit, model), bf),
            pltpu.VMEM((2, model, part_f), bf), pltpu.VMEM((2, part_f, model), bf),
            dma((2, 2)), dma((2, 2)), dma((2,)), dma((2 * per,)), dma((2 * per,)), dma((2,)), dma((2,)), dma((per,)), dma((per,)),
            dma((2,)), dma((2,)), dma((2,)), dma((2,)), dma((2,)), dma((2,)),
            dma((2, stages - 1)), dma((2,)), dma((2,)), dma((2, stages - 1)), dma((2,)), dma((2,)),
        ],
        compiler_params=pltpu.CompilerParams(collective_id=0, has_side_effects=True, vmem_limit_bytes=VMEM_BYTES),
        name='chain',
    )(x, g, w_in, w_out)


def solution(mesh):
    stages = mesh.shape['stage']
    replicas = mesh.shape['data']

    def local_fn(x, g, w_in, w_out):
        micro, tokens, model = x.shape
        y, dx, h_all, e_all, a_all, q_all, *_ = run_chain(
            x.reshape(micro * tokens, model), g.reshape(micro * tokens, model), w_in, w_out, stages, replicas)
        grad_first = jnp.einsum('vtd,vtf->vdf', h_all, q_all, preferred_element_type=jnp.float32)
        grad_second = jnp.einsum('vtf,vtd->vfd', a_all, e_all, preferred_element_type=jnp.float32)
        return y.reshape(x.shape), dx.reshape(x.shape), grad_first[:, None], grad_second[:, None]

    spec_rows = P(('part', 'data'))
    spec_weights = P(None, 'stage')
    spec_grads = P('part', 'stage')
    return jax.shard_map(local_fn, mesh=mesh, in_specs=(spec_rows, spec_rows, spec_weights, spec_weights), out_specs=(spec_rows, spec_rows, spec_grads, spec_grads), check_vma=False)
```

time: 231 us -> 211 us (0.913)
  Pallas kernels: 173 us -> 153 us
    pallas_call x1, Pallas kernels: 173 us -> 153 us  [run_chain(): pl.pallas_call(functools.partial(chain_kernel, stages, replicas, f_chunk)...]
where the time goes in v2:
time: 211 us
  Pallas kernels  153 us (73%)
  matrix products  55.3 us (26%)
    pallas_call x1, Pallas kernels, run_chain(): pl.pallas_call(functools.partial(chain_kernel, stages, replicas, f_chunk)...  153 us
    dot_general x1, matrix products, local_fn(): jnp.einsum('vtd,vtf->vdf', h_all, q_all, preferred_element_type=jnp.float32)  28.4 us
    dot_general x1, matrix products, local_fn(): jnp.einsum('vtf,vtd->vfd', a_all, e_all, preferred_element_type=jnp.float32)  26.9 us

profile of v2, /device:TPU:0, one launch (start us, length us, event | category | flops | bytes accessed | tf_op | source)
XLA Modules:
  0.0 210.8 jit_solution(7142041087208808845)
XLA Ops:
  0.6 153.3 %chain.1 = (bf16[256,1024]{1,0:T(8,128)(2,1)}, bf16[256,1024]{1,0:T(8,128)(2,1)}, bf16[2,1024,1024]{2,1,0:T(8,128)(2,1)}, bf16[2,1024,1024]{2,1,0:T(8,128)(2,1)}...) custom-call(bf16[256,1024]{1,0:T(8,128)(2,1)} %bitcast.16, ...), custom_call_target="tpu_custom_call" | custom-call | tf_op jit(solution)/shard_map/chain/pallas_call | solution.py:369
  153.9 28.4 %convolution_bitcast_fusion.1 = f32[2,1,1024,4096]{3,2,1,0:T(8,128)} fusion(bf16[2,1024,1024]{2,1,0:T(8,128)(2,1)} %get-tuple-element.12, bf16[2,1024,4096]{2,1,0:T(8,128)(2,1)} %get-tuple-element.13), kind=kOutput, calls=%fused_computation.1 | convolution fusion | flops 17179869184 | bytes 54525952 | tf_op jit(solution)/shard_map/vtd,vtf->vdf/dot_general | solution.py:400
  182.3 0.0 copy-start.1
  182.3 0.0 copy-start
  182.3 26.9 %convolution_bitcast_fusion = f32[2,1,4096,1024]{3,2,1,0:T(8,128)} fusion(bf16[2,1024,4096]{2,1,0:T(8,128)(2,1)} %get-tuple-element.14, bf16[2,1024,1024]{2,1,0:T(8,128)(2,1)} %get-tuple-element.15), kind=kOutput, calls=%fused_computation | convolution fusion | flops 17179869184 | bytes 54525952 | tf_op jit(solution)/shard_map/vtf,vtd->vfd/dot_general | solution.py:401
  209.2 0.0 copy-done.1
  209.2 0.8 copy.16
  210.0 0.0 copy-done
  210.0 0.8 copy.17
Async XLA Ops:
  182.3 26.9 %copy-start.1 = (bf16[256,1024]{1,0:T(8,128)(2,1)S(1)}, bf16[256,1024]{1,0:T(8,128)(2,1)}, u32[]{:S(2)}) copy-start(bf16[256,1024]{1,0:T(8,128)(2,1)} %get-tuple-element.10) | copy-start | bytes 1572868
  182.3 27.7 %copy-start = (bf16[256,1024]{1,0:T(8,128)(2,1)S(1)}, bf16[256,1024]{1,0:T(8,128)(2,1)}, u32[]{:S(2)}) copy-start(bf16[256,1024]{1,0:T(8,128)(2,1)} %get-tuple-element.11) | copy-start | bytes 1572868

commit v3 on v2

--- a/solution.py
+++ b/solution.py
@@ -24,10 +24,10 @@
 
 def chain_kernel(stages, replicas, f_chunk,
                  x_ref, g_ref, w_in_ref, w_out_ref,
-                 y_ref, dx_ref, h_out, e_out, a_out, q_out, slope_hbm, wide_hbm, tall_hbm,
-                 h_buf, e_buf, wide, tall, slope_buf, a_buf, q_buf, f_send_buf, b_send_buf, wide_stage, tall_stage,
+                 y_ref, dx_ref, ht_out, e_out, at_out, q_out, a_hbm, slope_hbm, wide_hbm, tall_hbm,
+                 h_buf, e_buf, wide, tall, slope_buf, a_buf, a_back, q_buf, f_send_buf, b_send_buf, wide_stage, tall_stage,
                  w_sem, wt_wr, wt_rd, f_recv, b_recv, f_send, b_send, x_send, g_send,
-                 slope_wr, slope_rd, a_wr, q_wr, h_wr, e_wr,
+                 slope_wr, slope_rd, a_wr, a_rd, q_wr, ht_wr, at_wr, e_wr,
                  y_send, y_loc, y_recv, d_send, d_loc, d_recv):
     stage = lax.axis_index('stage')
     data = lax.axis_index('data')
@@ -47,9 +47,8 @@
         return (pltpu.make_async_copy(w_in_ref.at[layer, 0], wide.at[layer], w_sem.at[layer, 0]),
                 pltpu.make_async_copy(w_out_ref.at[layer, 0], tall.at[layer], w_sem.at[layer, 1]))
 
-    for layer in range(2):
-        for copy in weight_copies(layer):
-            copy.start()
+    for copy in weight_copies(0):
+        copy.start()
 
     barrier = pltpu.get_barrier_semaphore()
     for off in range(1, stages):
@@ -100,7 +99,7 @@
     def f_writes(v, i):
         slot = lax.rem(i, 2)
         return (pltpu.make_async_copy(slope_buf.at[rows_of(2 + slot)], slope_hbm.at[v, rows_of(i)], slope_wr.at[slot]),
-                pltpu.make_async_copy(a_buf.at[slot], a_out.at[v, rows_of(i)], a_wr.at[slot]))
+                pltpu.make_async_copy(a_buf.at[slot], a_hbm.at[v, rows_of(i)], a_wr.at[slot]))
 
     def wt_writes(i):
         slot = lax.rem(i, 2)
@@ -132,6 +131,8 @@
 
     for copy in weight_copies(0):
         copy.wait()
+    for copy in weight_copies(1):
+        copy.start()
 
     def f_step_0(i, carry):
         @pl.when(i >= 2)
@@ -153,9 +154,10 @@
     for i in range(per - 2, per):
         f_hop(0, i).wait_send()
 
-    def slope_read(v, j):
+    def b_reads(v, j):
         slot = lax.rem(j, 2)
-        return pltpu.make_async_copy(slope_hbm.at[v, rows_of(j)], slope_buf.at[rows_of(slot)], slope_rd.at[slot])
+        return (pltpu.make_async_copy(slope_hbm.at[v, rows_of(j)], slope_buf.at[rows_of(slot)], slope_rd.at[slot]),
+                pltpu.make_async_copy(a_hbm.at[v, rows_of(j)], a_back.at[slot], a_rd.at[slot]))
 
     def f_step_1(i, carry):
         @pl.when(i < 2)
@@ -171,7 +173,8 @@
         for j in range(2):
             @pl.when(i == 2 + j)
             def _():
-                slope_read(1, j).start()
+                for copy in b_reads(1, j):
+                    copy.start()
 
         @pl.when(jnp.logical_and(i >= 2, jnp.logical_not(is_last)))
         def _():
@@ -208,15 +211,16 @@
         return (pltpu.make_async_copy(wide_hbm, wide.at[1], wt_rd.at[0]),
                 pltpu.make_async_copy(tall_hbm, tall.at[1], wt_rd.at[1]))
 
-    def h_copy(layer):
-        return pltpu.make_async_copy(h_buf.at[layer], h_out.at[layer], h_wr.at[layer])
-
     def e_copy(layer):
         return pltpu.make_async_copy(e_buf.at[layer], e_out.at[layer], e_wr.at[layer])
 
-    def q_write(v, j):
+    def b_writes(v, j):
         slot = lax.rem(j, 2)
-        return pltpu.make_async_copy(q_buf.at[slot], q_out.at[v, rows_of(j)], q_wr.at[slot])
+        turned = [pltpu.make_async_copy(
+            tall_stage.at[slot, :, pl.ds(c * unit, unit)], at_out.at[v, pl.ds(c * part_f, part_f), rows_of(j)],
+            at_wr.at[slot, c]) for c in range(per)]
+        return [pltpu.make_async_copy(q_buf.at[slot], q_out.at[v, rows_of(j)], q_wr.at[slot]),
+                pltpu.make_async_copy(wide_stage.at[slot, :, pl.ds(0, unit)], ht_out.at[v, :, rows_of(j)], ht_wr.at[slot])] + turned
 
     def b_hop(v, j):
         slot = lax.rem(j, 2)
@@ -247,21 +251,23 @@
             cols = pl.ds(c * f_chunk, f_chunk)
             d_act = jnp.dot(e_in, wide[1 - v, :, cols], preferred_element_type=jnp.float32)
             q_buf[slot, :, cols] = (slope_buf[rows_of(slot), cols] * d_act).astype(jnp.bfloat16)
+        for c in range(per):
+            tall_stage[slot, :, pl.ds(c * unit, unit)] = a_back[slot, :, pl.ds(c * part_f, part_f)].T
+        wide_stage[slot, :, pl.ds(0, unit)] = h_buf[v, rows_of(j), :].T
         if full:
             delta = jnp.dot(q_buf[slot], tall[1 - v], preferred_element_type=jnp.float32)
             b_send_buf[slot] = (e_in.astype(jnp.float32) + delta).astype(jnp.bfloat16)
 
     def b_step(n, carry):
         v, j = 1 - n // per, lax.rem(n, per)
-        slope_read(v, j).wait()
+        for copy in b_reads(v, j):
+            copy.wait()
 
         @pl.when(n == 1)
         def _():
             for i in range(per - 2, per):
                 for copy in f_writes(1, i):
                     copy.wait()
-            for layer in range(2):
-                h_copy(layer).start()
 
         @pl.when(n == per)
         def _():
@@ -272,7 +278,8 @@
         @pl.when(n >= 2)
         def _():
             back = n - 2
-            q_write(1 - back // per, lax.rem(back, per)).wait()
+            for copy in b_writes(1 - back // per, lax.rem(back, per)):
+                copy.wait()
 
         @pl.when(jnp.logical_and(n >= 2, hops(1 - (n - 2) // per)))
         def _():
@@ -280,6 +287,10 @@
 
         pltpu.make_async_copy(x_ref.at[pl.ds(0, unit)], e_buf.at[v, rows_of(j)], b_recv.at[n]).wait()
 
+        @pl.when(n == 2 * per - 1)
+        def _():
+            e_copy(0).start()
+
         @pl.when(jnp.logical_or(hops(v), j < 2))
         def _():
             b_compute(v, j, True)
@@ -292,12 +303,14 @@
         def _():
             b_hop(v, j).start()
 
-        q_write(v, j).start()
+        for copy in b_writes(v, j):
+            copy.start()
 
         @pl.when(n + 2 < 2 * per)
         def _():
             ahead = n + 2
-            slope_read(1 - ahead // per, lax.rem(ahead, per)).start()
+            for copy in b_reads(1 - ahead // per, lax.rem(ahead, per)):
+                copy.start()
 
         for k in range(2):
             @pl.when(jnp.logical_and(is_first, n == per + k))
@@ -309,9 +322,9 @@
         return carry
 
     lax.fori_loop(0, 2 * per, b_step, 0)
-    e_copy(0).start()
     for j in range(per - 2, per):
-        q_write(0, j).wait()
+        for copy in b_writes(0, j):
+            copy.wait()
 
     def share_done(src, dst, send_sem, recv_sem):
         for blk in range(1, replicas):
@@ -351,7 +364,6 @@
             pltpu.make_async_copy(f_send_buf.at[k], y_ref.at[pl.ds(k * unit, unit)], y_recv.at[k]).wait()
 
     for layer in range(2):
-        h_copy(layer).wait()
         e_copy(layer).wait()
 
 
@@ -369,19 +381,19 @@
     return pl.pallas_call(
         functools.partial(chain_kernel, stages, replicas, f_chunk),
         out_shape=(shape((rows, model), bf), shape((rows, model), bf),
-                   shape((2, total, model), bf), shape((2, total, model), bf),
-                   shape((2, total, hidden), bf), shape((2, total, hidden), bf),
-                   shape((2, total, hidden), f32), shape((model, hidden), bf), shape((hidden, model), bf)),
+                   shape((2, model, total), bf), shape((2, total, model), bf),
+                   shape((2, hidden, total), bf), shape((2, total, hidden), bf),
+                   shape((2, total, hidden), bf), shape((2, total, hidden), f32), shape((model, hidden), bf), shape((hidden, model), bf)),
         in_specs=[any_spec] * 4,
-        out_specs=(any_spec,) * 9,
+        out_specs=(any_spec,) * 10,
         scratch_shapes=[
             pltpu.VMEM((2, total, model), bf), pltpu.VMEM((2, total, model), bf),
             pltpu.VMEM((2, model, hidden), bf), pltpu.VMEM((2, hidden, model), bf),
-            pltpu.VMEM((4 * unit, hidden), f32), pltpu.VMEM((2, unit, hidden), bf), pltpu.VMEM((2, unit, hidden), bf),
+            pltpu.VMEM((4 * unit, hidden), f32), pltpu.VMEM((2, unit, hidden), bf), pltpu.VMEM((2, unit, hidden), bf), pltpu.VMEM((2, unit, hidden), bf),
             pltpu.VMEM((2, unit, model), bf), pltpu.VMEM((2, unit, model), bf),
             pltpu.VMEM((2, model, part_f), bf), pltpu.VMEM((2, part_f, model), bf),
             dma((2, 2)), dma((2, 2)), dma((2,)), dma((2 * per,)), dma((2 * per,)), dma((2,)), dma((2,)), dma((per,)), dma((per,)),
-            dma((2,)), dma((2,)), dma((2,)), dma((2,)), dma((2,)), dma((2,)),
+            dma((2,)), dma((2,)), dma((2,)), dma((2,)), dma((2,)), dma((2,)), dma((2, per)), dma((2,)),
             dma((2, stages - 1)), dma((2,)), dma((2,)), dma((2, stages - 1)), dma((2,)), dma((2,)),
         ],
         compiler_params=pltpu.CompilerParams(collective_id=0, has_side_effects=True, vmem_limit_bytes=VMEM_BYTES),
@@ -389,16 +401,39 @@
     )(x, g, w_in, w_out)
 
 
+def grad_kernel(ht_ref, q_ref, at_ref, e_ref, first_ref, second_ref):
+    first_ref[0] = jnp.dot(ht_ref[0], q_ref[0], preferred_element_type=jnp.float32)
+    second_ref[0] = jnp.dot(at_ref[0], e_ref[0], preferred_element_type=jnp.float32)
+
+
+def run_grads(ht, q, at, e):
+    layers, model, total = ht.shape
+    hidden = at.shape[1]
+    tile = hidden // 8
+    whole = lambda v, i: (v, 0, 0)
+    return pl.pallas_call(
+        grad_kernel,
+        grid=(layers, hidden // tile),
+        out_shape=(jax.ShapeDtypeStruct((layers, model, hidden), jnp.float32),
+                   jax.ShapeDtypeStruct((layers, hidden, model), jnp.float32)),
+        in_specs=[pl.BlockSpec((1, model, total), whole), pl.BlockSpec((1, total, tile), lambda v, i: (v, 0, i)),
+                  pl.BlockSpec((1, tile, total), lambda v, i: (v, i, 0)), pl.BlockSpec((1, total, model), whole)],
+        out_specs=(pl.BlockSpec((1, model, tile), lambda v, i: (v, 0, i)),
+                   pl.BlockSpec((1, tile, model), lambda v, i: (v, i, 0))),
+        compiler_params=pltpu.CompilerParams(dimension_semantics=('arbitrary', 'arbitrary'), vmem_limit_bytes=60_000_000),
+        name='grads',
+    )(ht, q, at, e)
+
+
 def solution(mesh):
     stages = mesh.shape['stage']
     replicas = mesh.shape['data']
 
     def local_fn(x, g, w_in, w_out):
         micro, tokens, model = x.shape
-        y, dx, h_all, e_all, a_all, q_all, *_ = run_chain(
+        y, dx, ht, e_all, at, q_all, *_ = run_chain(
             x.reshape(micro * tokens, model), g.reshape(micro * tokens, model), w_in, w_out, stages, replicas)
-        grad_first = jnp.einsum('vtd,vtf->vdf', h_all, q_all, preferred_element_type=jnp.float32)
-        grad_second = jnp.einsum('vtf,vtd->vfd', a_all, e_all, preferred_element_type=jnp.float32)
+        grad_first, grad_second = run_grads(ht, q_all, at, e_all)
         return y.reshape(x.shape), dx.reshape(x.shape), grad_first[:, None], grad_second[:, None]
 
     spec_rows = P(('part', 'data'))

time: 211 us -> 198 us (0.938)
  matrix products: 55.3 us -> 0 us
  Pallas kernels: 153 us -> 196 us
    dot_general x2 -> x0, matrix products: 55.3 us -> none  [the longest x1 28.4 us: local_fn(): jnp.einsum('vtd,vtf->vdf', h_all, q_all, preferred_element_type=jnp.float32)]
    pallas_call x0 -> x1, Pallas kernels: none -> 45.8 us  [run_grads(): pl.pallas_call(grad_kernel, grid=(layers, hidden // tile), out_shape=(jax...]
    pallas_call x1, Pallas kernels: 153 us -> 150 us  [run_chain(): pl.pallas_call(functools.partial(chain_kernel, stages, replicas, f_chunk)...]
where the time goes in v3:
time: 198 us
  Pallas kernels  196 us (99%)
    pallas_call x1, Pallas kernels, run_chain(): pl.pallas_call(functools.partial(chain_kernel, stages, replicas, f_chunk)...  150 us
    pallas_call x1, Pallas kernels, run_grads(): pl.pallas_call(grad_kernel, grid=(layers, hidden // tile), out_shape=(jax...  45.8 us

profile of v3, /device:TPU:0, one launch (start us, length us, event | category | flops | bytes accessed | tf_op | source)
XLA Modules:
  0.0 197.9 jit_solution(4746165348932662962)
XLA Ops:
  0.6 149.9 %chain.1 = (bf16[256,1024]{1,0:T(8,128)(2,1)}, bf16[256,1024]{1,0:T(8,128)(2,1)}, bf16[2,1024,1024]{2,1,0:T(8,128)(2,1)}, bf16[2,1024,1024]{2,1,0:T(8,128)(2,1)}...) custom-call(bf16[256,1024]{1,0:T(8,128)(2,1)} %bitcast.10, ...), custom_call_target="tpu_custom_call" | custom-call | tf_op jit(solution)/shard_map/chain/pallas_call | solution.py:381
  150.5 0.0 copy-start.1
  150.5 0.0 copy-start
  150.5 45.8 %grads.1 = (f32[2,1024,4096]{2,1,0:T(8,128)}, f32[2,4096,1024]{2,1,0:T(8,128)}) custom-call(bf16[2,1024,1024]{2,1,0:T(8,128)(2,1)} %get-tuple-element.14.ht_ref, bf16[2,1024,4096]{2,1,0:T(8,128)(2,1)} %get-tuple-element.15.q_ref, bf16[2,4096,1024]{2,1,0:T(8,128)(2,1)} %get-tuple-element.16.at_ref, bf16[2,1024,1024]{2,1,0:T(8,128)(2,1)} %get-tuple-element.17.e_ref), custom_call_target="tpu_custom_call" | custom-call | tf_op jit(solution)/shard_map/grads/pallas_call | solution.py:414
  196.3 0.0 copy-done.1
  196.3 0.8 copy.12
  197.1 0.0 copy-done
  197.1 0.8 copy.13
Async XLA Ops:
  150.5 45.8 %copy-start.1 = (bf16[256,1024]{1,0:T(8,128)(2,1)S(1)}, bf16[256,1024]{1,0:T(8,128)(2,1)}, u32[]{:S(2)}) copy-start(bf16[256,1024]{1,0:T(8,128)(2,1)} %get-tuple-element.12) | copy-start | bytes 1572868
  150.5 46.6 %copy-start = (bf16[256,1024]{1,0:T(8,128)(2,1)S(1)}, bf16[256,1024]{1,0:T(8,128)(2,1)}, u32[]{:S(2)}) copy-start(bf16[256,1024]{1,0:T(8,128)(2,1)} %get-tuple-element.13) | copy-start | bytes 1572868

commit v4 on v3

--- a/solution.py
+++ b/solution.py
@@ -47,8 +47,7 @@
         return (pltpu.make_async_copy(w_in_ref.at[layer, 0], wide.at[layer], w_sem.at[layer, 0]),
                 pltpu.make_async_copy(w_out_ref.at[layer, 0], tall.at[layer], w_sem.at[layer, 1]))
 
-    for copy in weight_copies(0):
-        copy.start()
+    weight_copies(0)[0].start()
 
     barrier = pltpu.get_barrier_semaphore()
     for off in range(1, stages):
@@ -106,7 +105,7 @@
         return (pltpu.make_async_copy(wide_stage.at[slot], wide_hbm.at[:, pl.ds(pl.multiple_of(i * part_f, part_f), part_f)], wt_wr.at[slot, 0]),
                 pltpu.make_async_copy(tall_stage.at[slot], tall_hbm.at[pl.ds(pl.multiple_of(i * part_f, part_f), part_f)], wt_wr.at[slot, 1]))
 
-    def f_compute(v, i, full):
+    def f_compute(v, i, full, before_second=None):
         slot = lax.rem(i, 2)
         h_in = h_buf[v, rows_of(i), :]
         for c in range(hidden // f_chunk):
@@ -115,6 +114,8 @@
             val, slope = gelu_pair(z)
             slope_buf[rows_of(2 + slot), cols] = slope
             a_buf[slot, :, cols] = val.astype(jnp.bfloat16)
+        if before_second is not None:
+            before_second()
         strip = pl.ds(pl.multiple_of(i * part_f, part_f), part_f)
         if v == 0:
             wide_stage[slot] = tall[v, strip, :].T
@@ -129,9 +130,17 @@
     def f_wait(v, i):
         pltpu.make_async_copy(x_ref.at[pl.ds(0, unit)], h_buf.at[v, rows_of(i)], f_recv.at[v * per + i]).wait()
 
-    for copy in weight_copies(0):
-        copy.wait()
-    for copy in weight_copies(1):
+    def second_weights():
+        weight_copies(0)[1].wait()
+        for copy in weight_copies(1):
+            copy.start()
+
+    weight_copies(0)[0].wait()
+    weight_copies(0)[1].start()
+    f_wait(0, 0)
+    f_compute(0, 0, True, second_weights)
+    f_hop(0, 0).start()
+    for copy in f_writes(0, 0) + wt_writes(0):
         copy.start()
 
     def f_step_0(i, carry):
@@ -148,7 +157,7 @@
             copy.start()
         return carry
 
-    lax.fori_loop(0, per, f_step_0, 0)
+    lax.fori_loop(1, per, f_step_0, 0)
     for copy in weight_copies(1):
         copy.wait()
     for i in range(per - 2, per):
@@ -401,28 +410,33 @@
     )(x, g, w_in, w_out)
 
 
-def grad_kernel(ht_ref, q_ref, at_ref, e_ref, first_ref, second_ref):
+def grad_kernel(ht_ref, q_ref, at_ref, e_ref, y_ref, dx_ref, first_ref, second_ref, y_out, dx_out):
+    y_out[...] = y_ref[...]
+    dx_out[...] = dx_ref[...]
     first_ref[0] = jnp.dot(ht_ref[0], q_ref[0], preferred_element_type=jnp.float32)
     second_ref[0] = jnp.dot(at_ref[0], e_ref[0], preferred_element_type=jnp.float32)
 
 
-def run_grads(ht, q, at, e):
+def run_grads(ht, q, at, e, y, dx):
     layers, model, total = ht.shape
     hidden = at.shape[1]
     tile = hidden // 8
+    rows = y.shape[0] // (layers * 8)
+    few = pl.BlockSpec((rows, model), lambda v, i: (v * 8 + i, 0))
     whole = lambda v, i: (v, 0, 0)
     return pl.pallas_call(
         grad_kernel,
         grid=(layers, hidden // tile),
         out_shape=(jax.ShapeDtypeStruct((layers, model, hidden), jnp.float32),
-                   jax.ShapeDtypeStruct((layers, hidden, model), jnp.float32)),
+                   jax.ShapeDtypeStruct((layers, hidden, model), jnp.float32),
+                   jax.ShapeDtypeStruct(y.shape, y.dtype), jax.ShapeDtypeStruct(dx.shape, dx.dtype)),
         in_specs=[pl.BlockSpec((1, model, total), whole), pl.BlockSpec((1, total, tile), lambda v, i: (v, 0, i)),
-                  pl.BlockSpec((1, tile, total), lambda v, i: (v, i, 0)), pl.BlockSpec((1, total, model), whole)],
+                  pl.BlockSpec((1, tile, total), lambda v, i: (v, i, 0)), pl.BlockSpec((1, total, model), whole), few, few],
         out_specs=(pl.BlockSpec((1, model, tile), lambda v, i: (v, 0, i)),
-                   pl.BlockSpec((1, tile, model), lambda v, i: (v, i, 0))),
+                   pl.BlockSpec((1, tile, model), lambda v, i: (v, i, 0)), few, few),
         compiler_params=pltpu.CompilerParams(dimension_semantics=('arbitrary', 'arbitrary'), vmem_limit_bytes=60_000_000),
         name='grads',
-    )(ht, q, at, e)
+    )(ht, q, at, e, y, dx)
 
 
 def solution(mesh):
@@ -433,7 +447,7 @@
         micro, tokens, model = x.shape
         y, dx, ht, e_all, at, q_all, *_ = run_chain(
             x.reshape(micro * tokens, model), g.reshape(micro * tokens, model), w_in, w_out, stages, replicas)
-        grad_first, grad_second = run_grads(ht, q_all, at, e_all)
+        grad_first, grad_second, y, dx = run_grads(ht, q_all, at, e_all, y, dx)
         return y.reshape(x.shape), dx.reshape(x.shape), grad_first[:, None], grad_second[:, None]
 
     spec_rows = P(('part', 'data'))

time: 198 us -> 199 us (level)
  no operation moved by 1% of the time
where the time goes in v4:
time: 199 us; the launch traced here: 198 us
  Pallas kernels  197 us (99%)
    pallas_call x1, Pallas kernels, run_chain(): pl.pallas_call(functools.partial(chain_kernel, stages, replicas, f_chunk)...  150 us
    pallas_call x1, Pallas kernels, run_grads(): pl.pallas_call(grad_kernel, grid=(layers, hidden // tile), out_shape=(jax...  47.6 us

profile of v4, /device:TPU:0, one launch (start us, length us, event | category | flops | bytes accessed | tf_op | source)
XLA Modules:
  0.0 198.2 jit_solution(3495998088603230736)
XLA Ops:
  0.6 149.9 %chain.1 = (bf16[256,1024]{1,0:T(8,128)(2,1)}, bf16[256,1024]{1,0:T(8,128)(2,1)}, bf16[2,1024,1024]{2,1,0:T(8,128)(2,1)}, bf16[2,1024,1024]{2,1,0:T(8,128)(2,1)}...) custom-call(bf16[256,1024]{1,0:T(8,128)(2,1)} %bitcast.10, ...), custom_call_target="tpu_custom_call" | custom-call | tf_op jit(solution)/shard_map/chain/pallas_call | solution.py:390
  150.5 47.6 %grads.1 = (f32[2,1024,4096]{2,1,0:T(8,128)}, f32[2,4096,1024]{2,1,0:T(8,128)}, bf16[256,1024]{1,0:T(8,128)(2,1)}, bf16[256,1024]{1,0:T(8,128)(2,1)}) custom-call(bf16[2,1024,1024]{2,1,0:T(8,128)(2,1)} %get-tuple-element.14.ht_ref, bf16[2,1024,4096]{2,1,0:T(8,128)(2,1)} %get-tuple-element.15.q_ref, bf16[2,4096,1024]{2,1,0:T(8,128)(2,1)} %get-tuple-element.16.at_ref, ...), custom_call_target="tpu_custom_call" | custom-call | tf_op jit(solution)/shard_map/grads/pallas_call | solution.py:427
